TPU v7x, 256 devices: a 4x2x16 block of a 4x16x16 slice. The times are simulated.
256 devices in a mesh: groups: 2 (over y), expert: 4 (over x), etp: 32 (over z, core).
Axes of the slice: x: 4, y: 2, z: 16, core: 2. Of those that a mesh axis runs over, the one named last changes fastest.
The devices are a block of a 4x16x16 slice.
Arguments:
- tokens: bfloat16 [1024, 4096], P(('groups', 'expert'), 'etp'), parts along dimension 0, may hold values from -6 to 6
- route_ids: int32 [1024, 2], P(('groups', 'expert')), parts along dimension 0, may hold values from 0 to 3, all different within a row; in each aligned block of 128 rows (0 to 127, 128 to 255, ...) at most 96 rows name the same one
- gate_weights: float32 [1024, 2], P(('groups', 'expert')), parts along dimension 0, may hold values from 0.2 to 1
- w_gate: bfloat16 [4, 4096, 14336], P('expert', None, 'etp'), may hold values from -0.09375 to 0.09375
- w_up: bfloat16 [4, 4096, 14336], P('expert', None, 'etp'), may hold values from -0.09375 to 0.09375
- w_down: bfloat16 [4, 14336, 4096], P('expert', 'etp'), may hold values from -0.09375 to 0.09375
Outputs:
- mixed: bfloat16 [1024, 4096], P(('groups', 'expert'), 'etp'), parts along dimension 0
There are 2 independent parts, one for each index of `groups`. A program takes and returns all parts, laid end to end along the dimension named above; an argument that names none is the same for every part. Nothing has to cross between parts.
Inputs may be any that keep to these rules, and one draw needn't show every extreme that they name: `route_ids`: each row names two different experts. In the rows of one index of expert (128 aligned rows), no expert is named by more than 96 rows, a bound that some block reaches.
All inputs are finite; a program needn't handle non-finite values.
Results may differ from a plain program's by a relative error of at most 0.024.
Values may be sent and summed in bfloat16 or wider, within the bound.
No kernel may reach another device: no remote copies, remote signals or barrier semaphores. Data moves between devices by JAX's collectives and lax.ppermute only.
A program may use at most 64 MiB of HBM per device.

v0:
```python
import jax
import jax.numpy as jnp
from jax import lax
from jax.sharding import Mesh
from jax.sharding import PartitionSpec as P

CAP = 96
ETP = ("etp_0", "etp_1")


def joined_along(tiles, dim):
    shape = list(tiles.shape[1:])
    shape[dim] *= tiles.shape[0]
    return jnp.moveaxis(tiles, 0, dim).reshape(shape)


def all_blocks(shard, axes, order):
    tiles = shard[None]
    for k in order:
        tiles = lax.all_gather(tiles, axes[k], axis=0, tiled=True)
    current = [lax.axis_size(axes[k]) for k in reversed(order)]
    tiles = tiles.reshape(*current, *shard.shape)
    turned = sorted(range(len(order)), key=lambda place: order[len(order) - 1 - place])
    return tiles.transpose(*turned, *range(len(order), tiles.ndim)).reshape(-1, *shard.shape)


def whole_of(shard, axes, order, dim):
    return joined_along(all_blocks(shard, axes, order), dim)


def cut_along(shard, dim, count):
    shape = shard.shape
    tiles = shard.reshape(*shape[:dim], count, shape[dim] // count, *shape[dim + 1 :])
    return jnp.moveaxis(tiles, dim, 0)


def sum_at_owner(shard, axis, dim):
    tiles = cut_along(shard, dim, lax.axis_size(axis))
    arrived = lax.all_to_all(tiles, axis, split_axis=0, concat_axis=0, tiled=True)
    return arrived.astype(jnp.float32).sum(axis=0)


def shards(tokens, route_ids, gate_weights, w_gate, w_up, w_down):
    cycle_size = lax.axis_size("expert")
    token_count, local_width = tokens.shape
    slot_total = cycle_size * CAP
    expert_iota = lax.broadcasted_iota(jnp.int32, (1, 1, cycle_size), 2)
    hit_mask = route_ids[:, :, None] == expert_iota
    routed = jnp.any(hit_mask, axis=1).astype(jnp.int32)
    weighting = jnp.sum(jnp.where(hit_mask, gate_weights[:, :, None], 0.0), axis=1)
    slot_index = jnp.cumsum(routed, axis=0) - 1
    expert_base = lax.broadcasted_iota(jnp.int32, (1, cycle_size), 1) * CAP
    target_slot = jnp.where(routed == 1, expert_base + slot_index, -1)
    slot_iota = lax.broadcasted_iota(jnp.int32, (1, 1, slot_total), 2)
    pick_table = target_slot[:, :, None] == slot_iota
    select_table = jnp.any(pick_table, axis=1).astype(jnp.bfloat16)
    combine_table = jnp.sum(jnp.where(pick_table, weighting[:, :, None], 0.0), axis=1)
    dispatched = jnp.dot(select_table.T, tokens, preferred_element_type=jnp.float32)
    dispatched = dispatched.astype(jnp.bfloat16).reshape(cycle_size, CAP, local_width)
    gate_local = w_gate[0]
    up_local = w_up[0]
    down_local = w_down[0]
    received = lax.all_to_all(dispatched, "expert", split_axis=0, concat_axis=0, tiled=True)
    columns_in = whole_of(received.reshape(slot_total, local_width), ETP, (0, 1), 1)
    gate_sum = jnp.dot(columns_in, gate_local, preferred_element_type=jnp.float32)
    up_sum = jnp.dot(columns_in, up_local, preferred_element_type=jnp.float32)
    hidden = (jax.nn.silu(gate_sum) * up_sum).astype(jnp.bfloat16)
    partial_out = jnp.dot(hidden, down_local, preferred_element_type=jnp.float32).astype(
        jnp.bfloat16
    )
    finished = sum_at_owner(partial_out, ETP, 1).astype(jnp.bfloat16)
    results = lax.all_to_all(
        finished.reshape(cycle_size, CAP, local_width),
        "expert",
        split_axis=0,
        concat_axis=0,
        tiled=True,
    )
    flat_results = results.reshape(slot_total, local_width).astype(jnp.float32)
    mixed = jnp.dot(combine_table, flat_results)
    return mixed.astype(jnp.bfloat16)


def solution(mesh):
    finer = Mesh(
        mesh.devices.reshape(mesh.shape["groups"], mesh.shape["expert"], 16, 2),
        ("groups", "expert", "etp_0", "etp_1"),
    )
    placed = (
        P(("groups", "expert"), ETP),
        P(("groups", "expert"), None),
        P(("groups", "expert"), None),
        P("expert", None, ETP),
        P("expert", None, ETP),
        P("expert", ETP, None),
    )
    return jax.shard_map(
        shards, mesh=finer, in_specs=placed, out_specs=P(("groups", "expert"), ETP), check_vma=False
    )
```

profile of v0, /device:TPU:160, one launch (start us, length us, event | category | flops | bytes accessed | tf_op | source)
XLA Modules:
  0.0 320.1 jit_solution(13523252470046150234)
XLA Ops:
  6.5 0.0 copy-start
  6.6 0.0 all-gather.3.cloned.1.call-start
  6.6 0.7 fusion.18
  7.3 0.1 copy.29
  7.4 0.2 reduce_window_sum.11
  7.6 0.1 copy.30
  7.6 0.1 add_select_fusion
  7.7 0.2 fusion.14
  7.9 0.0 copy-done
  7.9 0.3 convolution_convert_fusion.1
  8.1 10.3 %all_to_all.15 = bf16[4,96,128]{2,1,0:T(8,128)(2,1)} all-to-all(bf16[4,96,128]{2,1,0:T(8,128)(2,1)S(1)} %bitcast.49), channel_id=1, replica_groups=mesh['groups'=2,'expert'=4,'etp_0'=16,'etp_1'=2] {'expert'}, dimensions={0} | all-to-all | bytes 196608 | tf_op jit(solution)/shard_map/all_to_all | solution.py:63
  18.4 0.1 all-gather.3.cloned.1.call-update
  18.5 0.1 all-gather.5.cloned.1.call-start
  18.6 80.5 %all-gather.3.cloned.1.call-done = bf16[16,384,128]{2,1,0:T(8,128)(2,1)} async-done(((bf16[1,384,128]{2,1,0:T(8,128)(2,1)}), bf16[16,384,128]{2,1,0:T(8,128)(2,1)}) %all-gather.3.cloned.1.call-update) | async-done | bytes 1572880 | tf_op jit(solution)/shard_map/all_gather | solution.py:20
  99.1 0.1 all-gather.5.cloned.1.call-update
  99.1 19.8 %all-gather.5.cloned.1.call-done = bf16[32,384,128]{2,1,0:T(8,128)(2,1)} async-done(((bf16[16,384,128]{2,1,0:T(8,128)(2,1)}), bf16[32,384,128]{2,1,0:T(8,128)(2,1)}) %all-gather.5.cloned.1.call-update) | async-done | bytes 3145744 | tf_op jit(solution)/shard_map/all_gather | solution.py:20
  119.0 2.1 copy.31
  121.1 2.8 copy.32
  123.9 0.0 copy-start.1
  123.9 6.0 %fusion.3 = f32[384,448]{0,1:T(8,128)} fusion(bf16[384,4096]{0,1:T(8,128)(2,1)} %bitcast.45, bf16[1,4096,448]{1,2,0:T(8,128)(2,1)} %param.9), kind=kOutput, calls=%fused_computation.4 | convolution fusion | flops 1409286144 | bytes 7503872 | tf_op jit(solution)/shard_map/dot_general | solution.py:65
  130.0 0.0 copy-done.1
  130.0 8.9 %fusion.5 = bf16[48,32,8,128]{3,2,1,0:T(8,128)(2,1)} fusion(bf16[1,448,4096]{2,1,0:T(8,128)(2,1)} %param.11, bf16[384,4096]{0,1:T(8,128)(2,1)S(1)} %bitcast.46, bf16[1,4096,448]{1,2,0:T(8,128)(2,1)} %param.10, f32[384,448]{0,1:T(8,128)} %fusion.3), kind=kOutput, calls=%fused_computation.7 | convolution fusion | flops 2821177344 | bytes 14319616 | tf_op jit(solution)/shard_map/dot_general | solution.py:68
  138.8 4.5 %copy.36 = bf16[48,32,8,128]{3,2,0,1:T(8,128)(2,1)} copy(bf16[48,32,8,128]{3,2,1,0:T(8,128)(2,1)} %fusion.5) | data formatting | bytes 6291456 | tf_op jit(solution)/shard_map/reshape | solution.py:33
  143.3 0.0 copy-start.2
  143.3 0.0 copy-start.3
  143.3 13.0 %all-to-all-start.1 = ((bf16[32,384,128]{2,1,0:T(8,128)(2,1)}), bf16[32,384,128]{2,1,0:T(8,128)(2,1)S(1)}, u32[]{:S(2)}, u32[]{:S(2)}) async-start(bf16[32,384,128]{2,1,0:T(8,128)(2,1)} %bitcast.42), calls=%async_computation.1 | async-start | bytes 6291456 | tf_op jit(solution)/shard_map/all_to_all | solution.py:39
  156.4 0.0 copy-done.2
  156.4 0.0 copy-done.3
  156.4 144.9 %all-to-all-done.1 = bf16[32,384,128]{2,1,0:T(8,128)(2,1)S(1)} async-done(((bf16[32,384,128]{2,1,0:T(8,128)(2,1)}), bf16[32,384,128]{2,1,0:T(8,128)(2,1)S(1)}, u32[]{:S(2)}, u32[]{:S(2)}) %all-to-all-start.1) | async-done | bytes 3145760 | tf_op jit(solution)/shard_map/all_to_all | solution.py:39
  301.3 1.1 reduce_sum.32
  302.4 4.3 %all-to-all-start.2 = ((bf16[4,96,128]{2,1,0:T(8,128)(2,1)}), bf16[4,96,128]{2,1,0:T(8,128)(2,1)S(1)}, u32[]{:S(2)}, u32[]{:S(2)}) async-start(bf16[4,96,128]{2,1,0:T(8,128)(2,1)} %bitcast.11), calls=%async_computation.2 | async-start | bytes 196608 | tf_op jit(solution)/shard_map/all_to_all | solution.py:72
  306.7 0.2 select_reduce_fusion
  306.9 5.6 %all-to-all-done.2 = bf16[4,96,128]{2,1,0:T(8,128)(2,1)S(1)} async-done(((bf16[4,96,128]{2,1,0:T(8,128)(2,1)}), bf16[4,96,128]{2,1,0:T(8,128)(2,1)S(1)}, u32[]{:S(2)}, u32[]{:S(2)}) %all-to-all-start.2) | async-done | bytes 98336 | tf_op jit(solution)/shard_map/all_to_all | solution.py:72
  312.5 0.8 fusion.20
  (3 shorter events, 0.0 us)
Async XLA Ops:
  6.5 1.3 copy-start
  6.6 92.5 %all-gather.3.cloned.1.call-start = ((), (), s32[]{:S(2)}) async-start(), calls=%async_computation.3 | async-start | bytes 1671168 | tf_op jit(solution)/shard_map/all_gather | solution.py:20
  18.5 100.5 %all-gather.5.cloned.1.call-start = ((), (), s32[]{:S(2)}) async-start(), calls=%async_computation.4 | async-start | bytes 4718592 | tf_op jit(solution)/shard_map/all_gather | solution.py:20
  123.9 6.0 %copy-start.1 = (bf16[384,32,128]{0,2,1:T(8,128)(2,1)S(1)}, bf16[384,32,128]{0,2,1:T(8,128)(2,1)}, u32[]{:S(2)}) copy-start(bf16[384,32,128]{0,2,1:T(8,128)(2,1)} %copy.32) | copy-start | bytes 9437188
  143.3 13.1 %copy-start.2 = (f32[128,2]{0,1:T(2,128)S(1)}, f32[128,2]{0,1:T(2,128)}, u32[]{:S(2)}) copy-start(f32[128,2]{0,1:T(2,128)} %param.8) | copy-start | bytes 3076
  143.3 13.1 %copy-start.3 = (s32[128,2]{0,1:T(2,128)S(1)}, s32[128,2]{0,1:T(2,128)}, u32[]{:S(2)}) copy-start(s32[128,2]{0,1:T(2,128)} %param.7) | copy-start | bytes 3076
  143.3 158.0 %all-to-all-start.1 = ((bf16[32,384,128]{2,1,0:T(8,128)(2,1)}), bf16[32,384,128]{2,1,0:T(8,128)(2,1)S(1)}, u32[]{:S(2)}, u32[]{:S(2)}) async-start(bf16[32,384,128]{2,1,0:T(8,128)(2,1)} %bitcast.42), calls=%async_computation.1 | async-start | bytes 6291456 | tf_op jit(solution)/shard_map/all_to_all | solution.py:39
  302.4 10.1 %all-to-all-start.2 = ((bf16[4,96,128]{2,1,0:T(8,128)(2,1)}), bf16[4,96,128]{2,1,0:T(8,128)(2,1)S(1)}, u32[]{:S(2)}, u32[]{:S(2)}) async-start(bf16[4,96,128]{2,1,0:T(8,128)(2,1)} %bitcast.11), calls=%async_computation.2 | async-start | bytes 196608 | tf_op jit(solution)/shard_map/all_to_all | solution.py:72
Sparse Core Ops, SparseCore 0:
  18.6 80.4 all-gather.2
  100.9 18.0 all-gather.4
where the time goes:
time: 321 us; the launch traced here: 320 us
  waiting for transfers between devices  251 us (78%)
  starting transfers between devices  17.4 us (5%)
  matrix products  16 us (5%)
  between operations  13.5 us (4%)
  blocking collectives  10.3 us (3%)
  local copies, waits for them, and re-layouts  9.57 us (3%)
    all_to_all x1, waiting for transfers between devices, sum_at_owner(): lax.all_to_all(tiles, axis, split_axis=0, concat_axis=0, tiled=True)  145 us
    all_gather x2, waiting for transfers between devices, all_blocks(): tiles = lax.all_gather(tiles, axes[k], axis=0, tiled=True)  100 us
    all_to_all x1, starting transfers between devices, sum_at_owner(): lax.all_to_all(tiles, axis, split_axis=0, concat_axis=0, tiled=True)  13 us
    all_to_all x1, blocking collectives, shards(): lax.all_to_all(dispatched, 'expert', split_axis=0, concat_axis=0, tiled=T...  10.3 us
    dot_general x1, matrix products, shards(): jnp.dot(hidden, down_local, preferred_element_type=jnp.float32)  8.87 us
  transfers between devices with their start and end apart: 4, of which 4 were waited for; matrix products, arithmetic and copies ran while one was open for 0% of the time, Pallas kernels for 0%

commit v1 on v0

--- a/solution.py
+++ b/solution.py
@@ -17,7 +17,9 @@
 def all_blocks(shard, axes, order):
     tiles = shard[None]
     for k in order:
-        tiles = lax.all_gather(tiles, axes[k], axis=0, tiled=True)
+        tiles = jnp.concatenate(
+            lax.all_to_all(jnp.stack([tiles] * lax.axis_size(axes[k])), axes[k], 0, 0), axis=0
+        )
     current = [lax.axis_size(axes[k]) for k in reversed(order)]
     tiles = tiles.reshape(*current, *shard.shape)
     turned = sorted(range(len(order)), key=lambda place: order[len(order) - 1 - place])

time: 321 us -> 300 us (0.935)
  waiting for transfers between devices: 251 us -> 150 us
  blocking collectives: 10.3 us -> 111 us
  between operations: 13.5 us -> 0.09 us
  starting transfers between devices: 17.4 us -> 10.6 us
    all_to_all x0 -> x2, blocking collectives: none -> 101 us  [all_blocks(): lax.all_to_all(jnp.stack([tiles] * lax.axis_size(axes[k])), axes[k], 0, 0)]
    all_gather x2 -> x0, waiting for transfers between devices: 100 us -> none  [all_blocks(): tiles = lax.all_gather(tiles, axes[k], axis=0, tiled=True)]
    all_to_all x1, starting transfers between devices: 13 us -> 7.19 us  [sum_at_owner(): lax.all_to_all(tiles, axis, split_axis=0, concat_axis=0, tiled=True)]
  transfers between devices with their start and end apart: 4 -> 2, of which waited for: 4 -> 2; matrix products, arithmetic and copies ran while one was open for 0% -> 0% of each run, Pallas kernels for 0% -> 0%
where the time goes in v1:
time: 300 us; the launch traced here: 299 us
  waiting for transfers between devices  150 us (50%)
  blocking collectives  111 us (37%)
  matrix products  16 us (5%)
  starting transfers between devices  10.6 us (4%)
  local copies, waits for them, and re-layouts  7.97 us (3%)
    all_to_all x1, waiting for transfers between devices, sum_at_owner(): lax.all_to_all(tiles, axis, split_axis=0, concat_axis=0, tiled=True)  145 us
    all_to_all x2, blocking collectives, all_blocks(): lax.all_to_all(jnp.stack([tiles] * lax.axis_size(axes[k])), axes[k], 0, 0)  101 us
    all_to_all x1, blocking collectives, shards(): lax.all_to_all(dispatched, 'expert', split_axis=0, concat_axis=0, tiled=T...  10.2 us
    dot_general x1, matrix products, shards(): jnp.dot(hidden, down_local, preferred_element_type=jnp.float32)  8.89 us
    all_to_all x1, starting transfers between devices, sum_at_owner(): lax.all_to_all(tiles, axis, split_axis=0, concat_axis=0, tiled=True)  7.19 us
    dot_general x1, matrix products, shards(): jnp.dot(columns_in, gate_local, preferred_element_type=jnp.float32)  6.05 us
  transfers between devices with their start and end apart: 2, of which 2 were waited for; matrix products, arithmetic and copies ran while one was open for 0% of the time, Pallas kernels for 0%

profile of v1, /device:TPU:160, one launch (start us, length us, event | category | flops | bytes accessed | tf_op | source)
XLA Modules:
  0.0 299.2 jit_solution(2593261359349848149)
XLA Ops:
  0.0 0.0 copy-start
  0.0 0.7 fusion.18
  0.7 0.1 copy.25
  0.8 0.2 reduce_window_sum.11
  1.0 0.1 copy.26
  1.1 0.1 add_select_fusion
  1.1 0.2 fusion.14
  1.3 0.0 copy-done
  1.3 0.3 convolution_convert_fusion.1
  1.6 10.2 %all_to_all.25 = bf16[4,96,128]{2,1,0:T(8,128)(2,1)S(1)} all-to-all(bf16[4,96,128]{2,1,0:T(8,128)(2,1)S(1)} %bitcast.49), channel_id=1, replica_groups=mesh['groups'=2,'expert'=4,'etp_0'=16,'etp_1'=2] {'expert'}, dimensions={0} | all-to-all | bytes 196608 | tf_op jit(solution)/shard_map/all_to_all | solution.py:65
  11.8 0.3 stack.6
  12.1 95.0 %all_to_all.26 = bf16[16,1,384,128]{3,2,1,0:T(8,128)(2,1)S(1)} all-to-all(bf16[16,1,384,128]{3,2,1,0:T(8,128)(2,1)S(1)} %stack.6), channel_id=1, replica_groups=mesh['groups'=2,'expert'=4,'etp_0'=16,'etp_1'=2] {'etp_0'}, dimensions={0} | all-to-all | bytes 3145728 | tf_op jit(solution)/shard_map/all_to_all | solution.py:21
  107.1 0.3 pad_maximum_fusion
  107.4 6.3 %all_to_all.27 = bf16[2,16,384,128]{3,2,1,0:T(8,128)(2,1)S(1)} all-to-all(bf16[2,16,384,128]{3,2,1,0:T(8,128)(2,1)S(1)} %pad_maximum_fusion), channel_id=1, replica_groups=mesh['groups'=2,'expert'=4,'etp_0'=16,'etp_1'=2] {'etp_1'}, dimensions={0} | all-to-all | bytes 6291456 | tf_op jit(solution)/shard_map/all_to_all | solution.py:21
  113.6 0.2 copy.27
  113.9 2.8 copy.28
  116.7 0.0 copy-start.1
  116.7 6.1 %fusion.3 = f32[384,448]{0,1:T(8,128)} fusion(bf16[384,4096]{0,1:T(8,128)(2,1)} %bitcast.45, bf16[1,4096,448]{1,2,0:T(8,128)(2,1)} %param.9), kind=kOutput, calls=%fused_computation.4 | convolution fusion | flops 1409286144 | bytes 7503872 | tf_op jit(solution)/shard_map/dot_general | solution.py:67
  122.7 0.0 copy-done.1
  122.7 8.9 %fusion.5 = bf16[48,32,8,128]{3,2,1,0:T(8,128)(2,1)} fusion(bf16[1,448,4096]{2,1,0:T(8,128)(2,1)} %param.11, bf16[384,4096]{0,1:T(8,128)(2,1)S(1)} %bitcast.46, bf16[1,4096,448]{1,2,0:T(8,128)(2,1)} %param.10, f32[384,448]{0,1:T(8,128)} %fusion.3), kind=kOutput, calls=%fused_computation.8 | convolution fusion | flops 2821177344 | bytes 14319616 | tf_op jit(solution)/shard_map/dot_general | solution.py:70
  131.6 4.5 %copy.32 = bf16[48,32,8,128]{3,2,0,1:T(8,128)(2,1)} copy(bf16[48,32,8,128]{3,2,1,0:T(8,128)(2,1)} %fusion.5) | data formatting | bytes 6291456 | tf_op jit(solution)/shard_map/reshape | solution.py:35
  136.1 0.0 copy-start.2
  136.1 0.0 copy-start.3
  136.1 7.2 %all-to-all-start.3 = ((bf16[32,384,128]{2,1,0:T(8,128)(2,1)}), bf16[32,384,128]{2,1,0:T(8,128)(2,1)S(1)}, u32[]{:S(2)}, u32[]{:S(2)}) async-start(bf16[32,384,128]{2,1,0:T(8,128)(2,1)} %bitcast.42), calls=%async_computation.3 | async-start | bytes 6291456 | tf_op jit(solution)/shard_map/all_to_all | solution.py:41
  143.3 0.0 copy-done.2
  143.3 0.0 copy-done.3
  143.3 144.9 %all-to-all-done.3 = bf16[32,384,128]{2,1,0:T(8,128)(2,1)S(1)} async-done(((bf16[32,384,128]{2,1,0:T(8,128)(2,1)}), bf16[32,384,128]{2,1,0:T(8,128)(2,1)S(1)}, u32[]{:S(2)}, u32[]{:S(2)}) %all-to-all-start.3) | async-done | bytes 3145760 | tf_op jit(solution)/shard_map/all_to_all | solution.py:41
  288.2 1.1 reduce_sum.32
  289.3 3.4 %all-to-all-start.4 = ((bf16[4,96,128]{2,1,0:T(8,128)(2,1)}), bf16[4,96,128]{2,1,0:T(8,128)(2,1)S(1)}, u32[]{:S(2)}, u32[]{:S(2)}) async-start(bf16[4,96,128]{2,1,0:T(8,128)(2,1)} %bitcast.11), calls=%async_computation.4 | async-start | bytes 196608 | tf_op jit(solution)/shard_map/all_to_all | solution.py:74
  292.7 0.2 select_reduce_fusion
  292.9 5.5 %all-to-all-done.4 = bf16[4,96,128]{2,1,0:T(8,128)(2,1)S(1)} async-done(((bf16[4,96,128]{2,1,0:T(8,128)(2,1)}), bf16[4,96,128]{2,1,0:T(8,128)(2,1)S(1)}, u32[]{:S(2)}, u32[]{:S(2)}) %all-to-all-start.4) | async-done | bytes 98336 | tf_op jit(solution)/shard_map/all_to_all | solution.py:74
  298.4 0.8 fusion.20
  (3 shorter events, 0.0 us)
Async XLA Ops:
  0.0 1.3 copy-start
  116.7 6.1 %copy-start.1 = (bf16[384,32,128]{0,2,1:T(8,128)(2,1)S(1)}, bf16[384,32,128]{0,2,1:T(8,128)(2,1)}, u32[]{:S(2)}) copy-start(bf16[384,32,128]{0,2,1:T(8,128)(2,1)} %copy.28) | copy-start | bytes 9437188
  136.1 7.2 %copy-start.2 = (f32[128,2]{0,1:T(2,128)S(1)}, f32[128,2]{0,1:T(2,128)}, u32[]{:S(2)}) copy-start(f32[128,2]{0,1:T(2,128)} %param.8) | copy-start | bytes 3076
  136.1 7.2 %copy-start.3 = (s32[128,2]{0,1:T(2,128)S(1)}, s32[128,2]{0,1:T(2,128)}, u32[]{:S(2)}) copy-start(s32[128,2]{0,1:T(2,128)} %param.7) | copy-start | bytes 3076
  136.1 152.2 %all-to-all-start.3 = ((bf16[32,384,128]{2,1,0:T(8,128)(2,1)}), bf16[32,384,128]{2,1,0:T(8,128)(2,1)S(1)}, u32[]{:S(2)}, u32[]{:S(2)}) async-start(bf16[32,384,128]{2,1,0:T(8,128)(2,1)} %bitcast.42), calls=%async_computation.3 | async-start | bytes 6291456 | tf_op jit(solution)/shard_map/all_to_all | solution.py:41
  289.3 9.1 %all-to-all-start.4 = ((bf16[4,96,128]{2,1,0:T(8,128)(2,1)}), bf16[4,96,128]{2,1,0:T(8,128)(2,1)S(1)}, u32[]{:S(2)}, u32[]{:S(2)}) async-start(bf16[4,96,128]{2,1,0:T(8,128)(2,1)} %bitcast.11), calls=%async_computation.4 | async-start | bytes 196608 | tf_op jit(solution)/shard_map/all_to_all | solution.py:74
